TPU v7x, 256 devices: a whole 4x4x8 slice. The times are simulated.
256 devices in a mesh: fsdp: 32 (over z, x), rep: 8 (over y, core).
Axes of the slice: x: 4, y: 4, z: 8, core: 2. Of those that a mesh axis runs over, the one named last changes fastest.
Arguments:
- partials: bfloat16 [8, 112, 1024, 1024], P('rep', None, 'fsdp'), may hold values from -400 to 400
- sketch: bfloat16 [32, 8, 2, 1024, 256], P('fsdp', 'rep'), may hold values from -3 to 3
- owner_table: int32 [112, 1], replicated, may hold values from 0 to 31; in each aligned block of 14 rows (0 to 13, 14 to 27, ...) at most 2 rows name the same one
Outputs:
- update: bfloat16 [112, 1024, 1024], P('rep', 'fsdp')
- new_sketch: bfloat16 [32, 8, 2, 1024, 256], P('fsdp', 'rep')
Inputs may be any that keep to these rules, and one draw needn't show every extreme that they name: `owner_table`: in each aligned slice of 14 blocks no owner holds more than 2 blocks; some owner holds exactly 2 in some slice.
All inputs are finite; a program needn't handle non-finite values.
Results may differ from a plain program's by a relative error of at most 0.015.
Values may be sent and summed in bfloat16 or wider, within the bound.
A program may use at most 128 MiB of HBM per device.

v0:
```python
import functools
import math
import jax
import jax.numpy as jnp
from jax import lax
from jax.sharding import Mesh
from jax.sharding import PartitionSpec as P

NS_ITERS = 5
FSDP = ("fsdp_0", "fsdp_1")
REP = ("rep_0", "rep_1")
FSDP_REP = ("fsdp_0", "fsdp_1", "rep_0", "rep_1")
DECAY = 0.9
DAMPING = 64.0
FIRST_AXES = (((0,), (0,)), ((), ()))
LAST_AXES = (((1,), (1,)), ((), ()))


def one_axis_at_a_time(value, axes):
    return functools.reduce(lax.psum, axes, value)


def inverse_root(matrix, epsilon):
    identity = jnp.eye(matrix.shape[0], dtype=jnp.float32)
    trace_sum = jnp.trace(matrix) + epsilon
    current = matrix / trace_sum
    inverse = identity
    for repeat in range(NS_ITERS):
        middle = 1.5 * identity - 0.5 * jnp.dot(inverse, current, precision=lax.Precision.HIGHEST)
        current = jnp.dot(current, middle, precision=lax.Precision.HIGHEST)
        inverse = jnp.dot(middle, inverse, precision=lax.Precision.HIGHEST)
    return inverse / jnp.sqrt(trace_sum)


def precondition(gradient, current_sketch):
    identity = jnp.eye(current_sketch.shape[1], dtype=jnp.float32)
    projected = lax.dot_general(
        gradient, current_sketch, FIRST_AXES, preferred_element_type=jnp.float32
    ).astype(jnp.bfloat16)
    gram_matrix = lax.dot_general(
        current_sketch, current_sketch, FIRST_AXES, preferred_element_type=jnp.float32
    ).astype(jnp.bfloat16)
    powered = DECAY * jnp.dot(
        current_sketch, gram_matrix, preferred_element_type=jnp.float32
    ) + jnp.dot(gradient, projected, preferred_element_type=jnp.float32)
    inner_gram = lax.dot_general(powered, powered, FIRST_AXES, precision=lax.Precision.HIGHEST)
    basis_full = jnp.dot(powered, inverse_root(inner_gram, 1e-06), precision=lax.Precision.HIGHEST)
    basis_low = basis_full.astype(jnp.bfloat16)
    coefficients = lax.dot_general(
        gradient, basis_low, FIRST_AXES, preferred_element_type=jnp.float32
    ).astype(jnp.bfloat16)
    alignment = lax.dot_general(
        current_sketch, basis_low, FIRST_AXES, preferred_element_type=jnp.float32
    )
    energy = DECAY * lax.dot_general(
        alignment, alignment, FIRST_AXES, precision=lax.Precision.HIGHEST
    ) + lax.dot_general(coefficients, coefficients, FIRST_AXES, preferred_element_type=jnp.float32)
    root_inverse = inverse_root(energy + DAMPING * identity, 0.0)
    inner_part = jnp.dot(energy, root_inverse, precision=lax.Precision.HIGHEST)
    new_block = jnp.dot(basis_full, inner_part, precision=lax.Precision.HIGHEST).astype(
        jnp.bfloat16
    )
    mix_matrix = math.sqrt(DAMPING) * root_inverse - identity
    side_terms = lax.dot_general(
        coefficients.astype(jnp.float32), mix_matrix, LAST_AXES, precision=lax.Precision.HIGHEST
    ).astype(jnp.bfloat16)
    update_block = (
        gradient.astype(jnp.float32)
        + lax.dot_general(basis_low, side_terms, LAST_AXES, preferred_element_type=jnp.float32)
    ).astype(jnp.bfloat16)
    return (update_block, new_block)


def squared_sum(values):
    wide = values.astype(jnp.float32)
    return jnp.sum(wide * wide)


def process_slot(slot_index, arrived, clip_factor, held_sketches, filled):
    block_width = arrived.shape[-1]
    gradient = (clip_factor * arrived.reshape(block_width, block_width).astype(jnp.float32)).astype(
        jnp.bfloat16
    )
    current_sketch = held_sketches[slot_index]
    active = slot_index < filled
    update_block, new_block = precondition(gradient, current_sketch)
    new_block = jnp.where(active, new_block, current_sketch)
    return (update_block, new_block)


def local(partials, sketch, owner_table):
    block_total = partials.shape[1]
    row_count = partials.shape[2]
    block_width = partials.shape[3]
    fsdp_count = lax.axis_size(FSDP)
    per_slice = block_total // lax.axis_size(REP)
    slot_count = sketch.shape[2]
    reduced = lax.psum_scatter(
        partials[0].astype(jnp.float32).astype(jnp.bfloat16), REP, scatter_dimension=0, tiled=True
    )
    my_owners = lax.dynamic_slice_in_dim(
        owner_table[:, 0], lax.axis_index(REP) * per_slice, per_slice
    )
    positions = jnp.arange(per_slice, dtype=jnp.int32)
    same_owner = (my_owners[:, None] == my_owners[None, :]) & (
        positions[:, None] < positions[None, :]
    )
    rank_in = jnp.sum(same_owner.astype(jnp.int32), axis=0)
    target = rank_in * fsdp_count + my_owners
    selector = (
        target[None, :] == jnp.arange(slot_count * fsdp_count, dtype=jnp.int32)[:, None]
    ).astype(jnp.bfloat16)
    flattened = reduced.reshape(per_slice, row_count * block_width)
    outgoing = jnp.dot(selector, flattened, preferred_element_type=jnp.float32).astype(jnp.bfloat16)
    outgoing = outgoing.reshape(slot_count, fsdp_count, row_count, block_width)
    sum_squares = one_axis_at_a_time(squared_sum(reduced), FSDP_REP)
    clip_limit = 0.5 * math.sqrt(block_total * block_width * block_width)
    clip_factor = jnp.minimum(1.0, clip_limit / jnp.sqrt(sum_squares + 1e-06))
    filled = jnp.sum((my_owners == lax.axis_index(FSDP)).astype(jnp.int32))
    held_sketches = sketch[0, 0]
    fresh_list = []
    incoming = lax.all_to_all(outgoing, FSDP, split_axis=1, concat_axis=1, tiled=True)
    update_list = []
    for slot_index in range(slot_count):
        update_block, new_block = process_slot(
            slot_index, incoming[slot_index], clip_factor, held_sketches, filled
        )
        update_list.append(update_block)
        fresh_list.append(new_block)
    stacked = jnp.stack(update_list).reshape(slot_count, fsdp_count, row_count, block_width)
    returned = lax.all_to_all(stacked, FSDP, split_axis=1, concat_axis=1, tiled=True)
    returned = returned.reshape(slot_count * fsdp_count, row_count * block_width)
    my_updates = lax.dot_general(
        selector, returned, FIRST_AXES, preferred_element_type=jnp.float32
    ).astype(jnp.bfloat16)
    my_updates = my_updates.reshape(per_slice, row_count, block_width)
    return (my_updates, jnp.stack(fresh_list)[None, None])


def solution(mesh):
    torus = Mesh(mesh.devices.reshape(8, 4, 4, 2), ("fsdp_0", "fsdp_1", "rep_0", "rep_1"))
    return jax.shard_map(
        local,
        mesh=torus,
        in_specs=(P(REP, None, FSDP, None), P(FSDP, REP, None, None, None), P()),
        out_specs=(P(REP, FSDP, None), P(FSDP, REP, None, None, None)),
        check_vma=False,
    )
```

profile of v0, /device:TPU:3, one launch (start us, length us, event | category | flops | bytes accessed | tf_op | source)
XLA Modules:
  0.0 398.6 jit_solution(14725712927055801208)
XLA Ops:
  8.8 54.2 %reduce-scatter.2.cloned.1.call-done = bf16[14,32,1024]{2,1,0:T(8,128)(2,1)} async-done(((bf16[112,32,1024]{2,1,0:T(8,128)(2,1)}), bf16[14,32,1024]{2,1,0:T(8,128)(2,1)}) %reduce-scatter.2.cloned.1.call-update) | async-done | bytes 917520 | tf_op jit(solution)/shard_map/reduce_scatter | solution.py:98
  63.0 1.3 pad.4
  64.9 1.2 convolution_convert_fusion
  66.1 2.5 copy.27
  68.6 2.4 copy.18
  71.0 9.8 %all-to-all-start = ((bf16[2,32,32,1024]{3,2,0,1:T(8,128)(2,1)}), bf16[2,32,32,1024]{3,2,0,1:T(8,128)(2,1)}, u32[]{:S(2)}, u32[]{:S(2)}) async-start(bf16[2,32,32,1024]{3,2,0,1:T(8,128)(2,1)} %copy.18), calls=%async_computation.1 | async-start | bytes 8388608 | tf_op jit(solution)/shard_map/all_to_all | solution.py:122
  80.8 1.1 multiply_reduce_fusion
  81.8 98.5 %psum.28 = f32[]{:T(128)} all-reduce(f32[]{:T(128)} %multiply_reduce_fusion), channel_id=1, replica_groups=mesh['fsdp_0'=8,'fsdp_1'=4,'rep_0'=4,'rep_1'=2] {'fsdp_0'}, use_global_device_ids=true, to_apply=%region_3.0 | all-reduce | flops 1 | bytes 8 | tf_op jit(solution)/shard_map/psum | solution.py:20
  180.3 7.4 %psum.29 = f32[]{:T(128)} all-reduce(f32[]{:T(128)} %psum.28), channel_id=1, replica_groups=mesh['fsdp_0'=8,'fsdp_1'=4,'rep_0'=4,'rep_1'=2] {'fsdp_1'}, use_global_device_ids=true, to_apply=%region_4.0 | all-reduce | flops 1 | bytes 8 | tf_op jit(solution)/shard_map/psum | solution.py:20
  187.8 11.2 %psum.30 = f32[]{:T(128)} all-reduce(f32[]{:T(128)} %psum.29), channel_id=1, replica_groups=mesh['fsdp_0'=8,'fsdp_1'=4,'rep_0'=4,'rep_1'=2] {'rep_0'}, use_global_device_ids=true, to_apply=%region_5.0 | all-reduce | flops 1 | bytes 8 | tf_op jit(solution)/shard_map/psum | solution.py:20
  199.0 10.0 %psum.31 = f32[]{:T(128)} all-reduce(f32[]{:T(128)} %psum.30), channel_id=1, replica_groups=mesh['fsdp_0'=8,'fsdp_1'=4,'rep_0'=4,'rep_1'=2] {'rep_1'}, use_global_device_ids=true, to_apply=%region_6.0 | all-reduce | flops 1 | bytes 8 | tf_op jit(solution)/shard_map/psum | solution.py:20
  209.7 5.0 %multiply_convert_fusion.1 = (bf16[1,32,32,1024]{3,2,0,1:T(8,128)(2,1)}, bf16[1,32,32,1024]{3,2,0,1:T(8,128)(2,1)S(1)}) fusion(bf16[2,32,32,1024]{3,2,0,1:T(8,128)(2,1)} %all-to-all-done, f32[]{:T(128)S(6)} %min_shard_map.3), kind=kLoop, calls=%fused_computation.6 | loop fusion | flops 6291456 | bytes 8388612 | tf_op jit(solution)/shard_map/convert_element_type | solution.py:81
  214.7 1.3 copy-done.5
  216.0 3.3 fusion.11
  219.3 2.1 fusion.1
  221.4 1.6 select_reduce_fusion.1
  229.0 1.8 fusion.92
  240.4 1.1 fusion.99
  241.5 5.5 %fusion.10 = f32[1024,256]{0,1:T(8,128)} fusion(bf16[1024,1024]{1,0:T(8,128)(2,1)} %bitcast.194, bf16[1,1,2,1024,256]{4,3,2,1,0:T(8,128)(2,1)S(1)} %copy-done), kind=kOutput, calls=%fused_computation.76 | convolution fusion | flops 1074003968 | bytes 5767168 | tf_op jit(solution)/shard_map/dot_general | solution.py:45
  247.0 2.1 fusion.3
  249.0 2.3 select_reduce_fusion.3
  252.1 1.3 select_subtract_fusion.19
  253.3 1.3 fusion.44
  259.6 1.8 fusion.78
  263.4 1.0 select_reduce_fusion.2
  276.3 2.3 pad_maximum_fusion
  278.7 7.0 %all-to-all-start.1 = ((bf16[2,32,32,1024]{3,2,0,1:T(8,128)(2,1)}), bf16[2,32,32,1024]{3,2,0,1:T(8,128)(2,1)}, u32[]{:S(2)}, u32[]{:S(2)}) async-start(bf16[2,32,32,1024]{3,2,0,1:T(8,128)(2,1)} %pad_maximum_fusion), calls=%async_computation.2 | async-start | bytes 8388608 | tf_op jit(solution)/shard_map/all_to_all | solution.py:131
  287.0 1.4 fusion.101
  290.8 1.1 maximum_bitcast_fusion
  291.9 92.1 %all-to-all-done.1 = bf16[2,32,32,1024]{3,2,0,1:T(8,128)(2,1)} async-done(((bf16[2,32,32,1024]{3,2,0,1:T(8,128)(2,1)}), bf16[2,32,32,1024]{3,2,0,1:T(8,128)(2,1)}, u32[]{:S(2)}, u32[]{:S(2)}) %all-to-all-start.1) | async-done | bytes 4194336 | tf_op jit(solution)/shard_map/all_to_all | solution.py:131
  384.0 2.6 copy.23
  386.6 2.6 copy.28
  (120 shorter events, 38.5 us)
Async XLA Ops:
  7.2 55.8 %reduce-scatter.2.cloned.1.call-start = ((), (), s32[]{:S(2)}) async-start(), calls=%async_computation.3 | async-start | bytes 8257536 | tf_op jit(solution)/shard_map/reduce_scatter | solution.py:98
  7.2 0.7 copy-start.21
  71.0 9.8 %copy-start.12 = (bf16[14,32,1024]{2,1,0:T(8,128)(2,1)S(1)}, bf16[14,32,1024]{2,1,0:T(8,128)(2,1)}, u32[]{:S(2)}) copy-start(bf16[14,32,1024]{2,1,0:T(8,128)(2,1)} %reduce-scatter.2.cloned.1.call-done) | copy-start | bytes 2752516
  71.0 138.7 %all-to-all-start = ((bf16[2,32,32,1024]{3,2,0,1:T(8,128)(2,1)}), bf16[2,32,32,1024]{3,2,0,1:T(8,128)(2,1)}, u32[]{:S(2)}, u32[]{:S(2)}) async-start(bf16[2,32,32,1024]{3,2,0,1:T(8,128)(2,1)} %copy.18), calls=%async_computation.1 | async-start | bytes 8388608 | tf_op jit(solution)/shard_map/all_to_all | solution.py:122
  209.7 6.4 %copy-start = (bf16[1,1,2,1024,256]{4,3,2,1,0:T(8,128)(2,1)S(1)}, bf16[1,1,2,1024,256]{4,3,2,1,0:T(8,128)(2,1)}, u32[]{:S(2)}) copy-start(bf16[1,1,2,1024,256]{4,3,2,1,0:T(8,128)(2,1)} %param.4) | copy-start | bytes 3145732
  214.7 1.4 copy-start.5
  228.9 2.2 copy-start.6
  232.1 0.8 copy-start.8
  234.3 3.8 copy-start.18
  259.6 2.2 copy-start.3
  261.5 1.1 copy-start.1
  262.6 0.8 copy-start.10
  264.5 3.8 copy-start.19
  269.0 2.0 copy-start.13
  269.8 2.7 copy-start.9
  270.6 2.6 copy-start.7
  271.8 0.7 copy-start.14
  273.1 1.7 copy-start.11
  273.1 2.4 copy-start.4
  273.9 1.6 copy-start.2
  274.9 1.4 copy-start.16
  278.6 8.4 %copy-start.15 = (f32[256,256]{1,0:T(8,128)S(1)}, f32[256,256]{1,0:T(8,128)}, u32[]{:S(2)}) copy-start(f32[256,256]{1,0:T(8,128)} %copy-done.14) | copy-start | bytes 786436
  278.7 105.4 %all-to-all-start.1 = ((bf16[2,32,32,1024]{3,2,0,1:T(8,128)(2,1)}), bf16[2,32,32,1024]{3,2,0,1:T(8,128)(2,1)}, u32[]{:S(2)}, u32[]{:S(2)}) async-start(bf16[2,32,32,1024]{3,2,0,1:T(8,128)(2,1)} %pad_maximum_fusion), calls=%async_computation.2 | async-start | bytes 8388608 | tf_op jit(solution)/shard_map/all_to_all | solution.py:131
  287.0 2.4 copy-start.17
  287.0 2.4 copy-start.20
Sparse Core Ops, SparseCore 0:
  10.5 52.4 reduce-scatter.1
where the time goes:
time: 404 us; the launch traced here: 399 us
  waiting for transfers between devices  147 us (36%)
  blocking collectives  127 us (31%)
  matrix products  60.5 us (15%)
  between operations  19.9 us (5%)
  local copies, waits for them, and re-layouts  17 us (4%)
  starting transfers between devices  16.8 us (4%)
  other arithmetic  10.3 us (3%)
    psum x4, blocking collectives, one_axis_at_a_time(): return functools.reduce(lax.psum, axes, value)  127 us
    all_to_all x1, waiting for transfers between devices, local(): lax.all_to_all(stacked, FSDP, split_axis=1, concat_axis=1, tiled=True)  92.1 us
    reduce_scatter x1, waiting for transfers between devices, local(): lax.psum_scatter(partials[0].astype(jnp.float32).astype(jnp.bfloat16), RE...  54.2 us
    unnamed x49, local copies, waits for them, and re-layouts  10.9 us
    dot_general x20, matrix products, inverse_root(): jnp.dot(inverse, current, precision=lax.Precision.HIGHEST)  10 us
    all_to_all x1, starting transfers between devices, local(): lax.all_to_all(outgoing, FSDP, split_axis=1, concat_axis=1, tiled=True)  9.76 us
    dot_general x16, matrix products, inverse_root(): current = jnp.dot(current, middle, precision=lax.Precision.HIGHEST)  9.04 us
    dot_general x2, matrix products, precondition(): jnp.dot(gradient, projected, preferred_element_type=jnp.float32)  8.72 us
  transfers between devices with their start and end apart: 3, of which 2 were waited for; matrix products, arithmetic and copies ran while one was open for 2% of the time, Pallas kernels for 0%

commit v1 on v0

--- a/solution.py
+++ b/solution.py
@@ -119,7 +119,10 @@
     filled = jnp.sum((my_owners == lax.axis_index(FSDP)).astype(jnp.int32))
     held_sketches = sketch[0, 0]
     fresh_list = []
-    incoming = lax.all_to_all(outgoing, FSDP, split_axis=1, concat_axis=1, tiled=True)
+    incoming = jnp.concatenate(
+        lax.all_to_all(jnp.stack(jnp.split(outgoing, lax.axis_size(FSDP), axis=1)), FSDP, 0, 0),
+        axis=1,
+    )
     update_list = []
     for slot_index in range(slot_count):
         update_block, new_block = process_slot(

time: 404 us -> 422 us (1.045)
  local copies, waits for them, and re-layouts: 17 us -> 33.9 us
    unnamed x49 -> x74, local copies, waits for them, and re-layouts: 10.9 us -> 29.6 us
where the time goes in v1:
time: 422 us; the launch traced here: 416 us
  waiting for transfers between devices  146 us (35%)
  blocking collectives  127 us (30%)
  matrix products  61.4 us (15%)
  local copies, waits for them, and re-layouts  33.9 us (8%)
  between operations  20 us (5%)
  starting transfers between devices  17 us (4%)
  other arithmetic  11 us (3%)
    psum x4, blocking collectives, one_axis_at_a_time(): return functools.reduce(lax.psum, axes, value)  127 us
    all_to_all x1, waiting for transfers between devices, local(): lax.all_to_all(stacked, FSDP, split_axis=1, concat_axis=1, tiled=True)  91.2 us
    reduce_scatter x1, waiting for transfers between devices, local(): lax.psum_scatter(partials[0].astype(jnp.float32).astype(jnp.bfloat16), RE...  54.2 us
    unnamed x74, local copies, waits for them, and re-layouts  29.6 us
    dot_general x20, matrix products, inverse_root(): jnp.dot(inverse, current, precision=lax.Precision.HIGHEST)  10 us
    dot_general x2, matrix products, precondition(): jnp.dot(gradient, projected, preferred_element_type=jnp.float32)  9.97 us
    all_to_all x1, starting transfers between devices, local(): lax.all_to_all(jnp.stack(jnp.split(outgoing, lax.axis_size(FSDP), axis=1)...  9.76 us
    dot_general x16, matrix products, inverse_root(): current = jnp.dot(current, middle, precision=lax.Precision.HIGHEST)  9.08 us
  transfers between devices with their start and end apart: 3, of which 2 were waited for; matrix products, arithmetic and copies ran while one was open for 2% of the time, Pallas kernels for 0%

profile of v1, /device:TPU:3, one launch (start us, length us, event | category | flops | bytes accessed | tf_op | source)
XLA Modules:
  0.0 416.4 jit_solution(4353835154653293186)
XLA Ops:
  8.8 54.2 %reduce-scatter.2.cloned.1.call-done = bf16[14,32,1024]{2,1,0:T(8,128)(2,1)} async-done(((bf16[112,32,1024]{2,1,0:T(8,128)(2,1)}), bf16[14,32,1024]{2,1,0:T(8,128)(2,1)}) %reduce-scatter.2.cloned.1.call-update) | async-done | bytes 917520 | tf_op jit(solution)/shard_map/reduce_scatter | solution.py:98
  63.0 1.3 pad.4
  64.9 1.2 convolution_convert_fusion
  66.1 2.5 copy.179
  89.7 9.8 %all-to-all-start = ((bf16[32,2,1,32,1024]{4,3,1,2,0:T(8,128)(2,1)}), bf16[32,2,1,32,1024]{4,3,1,2,0:T(8,128)(2,1)}, u32[]{:S(2)}, u32[]{:S(2)}) async-start(bf16[32,2,1,32,1024]{4,3,1,2,0:T(8,128)(2,1)} %fusion.42), calls=%async_computation.1 | async-start | bytes 8388608 | tf_op jit(solution)/shard_map/all_to_all | solution.py:123
  99.4 1.1 multiply_reduce_fusion
  100.5 98.5 %psum.28 = f32[]{:T(128)} all-reduce(f32[]{:T(128)} %multiply_reduce_fusion), channel_id=1, replica_groups=mesh['fsdp_0'=8,'fsdp_1'=4,'rep_0'=4,'rep_1'=2] {'fsdp_0'}, use_global_device_ids=true, to_apply=%region_3.0 | all-reduce | flops 1 | bytes 8 | tf_op jit(solution)/shard_map/psum | solution.py:20
  199.0 7.4 %psum.29 = f32[]{:T(128)} all-reduce(f32[]{:T(128)} %psum.28), channel_id=1, replica_groups=mesh['fsdp_0'=8,'fsdp_1'=4,'rep_0'=4,'rep_1'=2] {'fsdp_1'}, use_global_device_ids=true, to_apply=%region_4.0 | all-reduce | flops 1 | bytes 8 | tf_op jit(solution)/shard_map/psum | solution.py:20
  206.4 11.2 %psum.30 = f32[]{:T(128)} all-reduce(f32[]{:T(128)} %psum.29), channel_id=1, replica_groups=mesh['fsdp_0'=8,'fsdp_1'=4,'rep_0'=4,'rep_1'=2] {'rep_0'}, use_global_device_ids=true, to_apply=%region_5.0 | all-reduce | flops 1 | bytes 8 | tf_op jit(solution)/shard_map/psum | solution.py:20
  217.6 9.8 %psum.31 = f32[]{:T(128)} all-reduce(f32[]{:T(128)} %psum.30), channel_id=1, replica_groups=mesh['fsdp_0'=8,'fsdp_1'=4,'rep_0'=4,'rep_1'=2] {'rep_1'}, use_global_device_ids=true, to_apply=%region_6.0 | all-reduce | flops 1 | bytes 8 | tf_op jit(solution)/shard_map/psum | solution.py:20
  228.2 5.7 %multiply_convert_fusion.1 = (bf16[1,32,1,32,1024]{4,3,0,2,1:T(8,128)(2,1)}, bf16[1,32,1,32,1024]{4,3,0,2,1:T(8,128)(2,1)}) fusion(bf16[2,32,1,32,1024]{4,3,0,2,1:T(8,128)(2,1)} %bitcast.34, f32[]{:T(128)S(6)} %min_shard_map.3), kind=kLoop, calls=%fused_computation.6 | loop fusion | flops 6291456 | bytes 8388612 | tf_op jit(solution)/shard_map/convert_element_type | solution.py:81
  233.9 4.5 %fusion.11 = f32[1024,256]{0,1:T(8,128)S(1)} fusion(bf16[1024,1024]{1,0:T(8,128)(2,1)} %bitcast.419, bf16[1,1,2,1024,256]{4,3,2,1,0:T(8,128)(2,1)S(1)} %copy-done), kind=kOutput, calls=%fused_computation.77 | convolution fusion | flops 1074003968 | bytes 5767168 | tf_op jit(solution)/shard_map/dot_general | solution.py:45
  239.2 1.6 select_reduce_fusion.1
  246.8 1.8 fusion.124
  253.9 1.0 fusion.78
  258.3 1.1 fusion.131
  259.4 5.5 %fusion.10 = f32[1024,256]{0,1:T(8,128)} fusion(bf16[1024,1024]{1,0:T(8,128)(2,1)} %bitcast.416, bf16[1,1,2,1024,256]{4,3,2,1,0:T(8,128)(2,1)S(1)} %copy-done), kind=kOutput, calls=%fused_computation.76 | convolution fusion | flops 1074003968 | bytes 5767168 | tf_op jit(solution)/shard_map/dot_general | solution.py:45
  264.9 2.1 fusion.3
  266.9 2.4 select_reduce_fusion.3
  270.1 1.3 select_subtract_fusion.19
  271.4 1.3 fusion.76
  277.7 1.8 fusion.110
  281.0 1.0 select_reduce_fusion.2
  283.7 1.1 fusion.81
  293.9 2.3 pad_maximum_fusion
  296.3 7.2 %all-to-all-start.1 = ((bf16[2,32,32,1024]{3,2,0,1:T(8,128)(2,1)}), bf16[2,32,32,1024]{3,2,0,1:T(8,128)(2,1)}, u32[]{:S(2)}, u32[]{:S(2)}) async-start(bf16[2,32,32,1024]{3,2,0,1:T(8,128)(2,1)} %pad_maximum_fusion), calls=%async_computation.2 | async-start | bytes 8388608 | tf_op jit(solution)/shard_map/all_to_all | solution.py:134
  304.9 1.3 fusion.133
  307.2 1.4 fusion.132
  309.6 1.1 maximum_bitcast_fusion
  310.7 91.2 %all-to-all-done.1 = bf16[2,32,32,1024]{3,2,0,1:T(8,128)(2,1)} async-done(((bf16[2,32,32,1024]{3,2,0,1:T(8,128)(2,1)}), bf16[2,32,32,1024]{3,2,0,1:T(8,128)(2,1)}, u32[]{:S(2)}, u32[]{:S(2)}) %all-to-all-start.1) | async-done | bytes 4194336 | tf_op jit(solution)/shard_map/all_to_all | solution.py:134
  401.8 2.6 copy.144
  404.5 2.6 copy.180
  (145 shorter events, 57.5 us)
Async XLA Ops:
  7.2 0.8 copy-start.18
  7.2 55.8 %reduce-scatter.2.cloned.1.call-start = ((), (), s32[]{:S(2)}) async-start(), calls=%async_computation.3 | async-start | bytes 8257536 | tf_op jit(solution)/shard_map/reduce_scatter | solution.py:98
  89.7 9.8 %copy-start.11 = (bf16[14,32,1024]{2,1,0:T(8,128)(2,1)S(1)}, bf16[14,32,1024]{2,1,0:T(8,128)(2,1)}, u32[]{:S(2)}) copy-start(bf16[14,32,1024]{2,1,0:T(8,128)(2,1)} %reduce-scatter.2.cloned.1.call-done) | copy-start | bytes 2752516
  89.7 138.5 %all-to-all-start = ((bf16[32,2,1,32,1024]{4,3,1,2,0:T(8,128)(2,1)}), bf16[32,2,1,32,1024]{4,3,1,2,0:T(8,128)(2,1)}, u32[]{:S(2)}, u32[]{:S(2)}) async-start(bf16[32,2,1,32,1024]{4,3,1,2,0:T(8,128)(2,1)} %fusion.42), calls=%async_computation.1 | async-start | bytes 8388608 | tf_op jit(solution)/shard_map/all_to_all | solution.py:123
  228.2 5.7 %copy-start = (bf16[1,1,2,1024,256]{4,3,2,1,0:T(8,128)(2,1)S(1)}, bf16[1,1,2,1024,256]{4,3,2,1,0:T(8,128)(2,1)}, u32[]{:S(2)}) copy-start(bf16[1,1,2,1024,256]{4,3,2,1,0:T(8,128)(2,1)} %param.4) | copy-start | bytes 3145732
  244.9 4.1 copy-start.5
  250.0 0.8 copy-start.7
  252.2 5.7 %copy-start.16 = (f32[256,256]{1,0:T(8,128)}, f32[256,256]{1,0:T(8,128)S(1)}, u32[]{:S(2)}) copy-start(f32[256,256]{1,0:T(8,128)S(1)} %get-tuple-element.9) | copy-start | bytes 786436
  275.3 4.5 %copy-start.3 = (bf16[1,32,1,32,1024]{4,3,0,2,1:T(8,128)(2,1)S(1)}, bf16[1,32,1,32,1024]{4,3,0,2,1:T(8,128)(2,1)}, u32[]{:S(2)}) copy-start(bf16[1,32,1,32,1024]{4,3,0,2,1:T(8,128)(2,1)} %get-tuple-element.4) | copy-start | bytes 6291460
  279.5 1.5 copy-start.1
  280.6 1.4 copy-start.9
  282.1 5.8 %copy-start.17 = (f32[256,256]{1,0:T(8,128)}, f32[256,256]{1,0:T(8,128)S(1)}, u32[]{:S(2)}) copy-start(f32[256,256]{1,0:T(8,128)S(1)} %get-tuple-element.13) | copy-start | bytes 786436
  283.7 4.9 %copy-start.12 = (f32[256,256]{1,0:T(8,128)S(1)}, f32[256,256]{1,0:T(8,128)}, u32[]{:S(2)}) copy-start(f32[256,256]{1,0:T(8,128)} %fusion.131) | copy-start | bytes 786436
  285.5 4.6 %copy-start.8 = (bf16[1024,256]{1,0:T(8,128)(2,1)S(1)}, bf16[1024,256]{1,0:T(8,128)(2,1)}, u32[]{:S(2)}) copy-start(bf16[1024,256]{1,0:T(8,128)(2,1)} %copy-done.7) | copy-start | bytes 1572868
  285.9 4.9 %copy-start.6 = (bf16[1,32,1,32,1024]{4,3,0,2,1:T(8,128)(2,1)S(1)}, bf16[1,32,1,32,1024]{4,3,0,2,1:T(8,128)(2,1)}, u32[]{:S(2)}) copy-start(bf16[1,32,1,32,1024]{4,3,0,2,1:T(8,128)(2,1)} %get-tuple-element.5) | copy-start | bytes 6291460
  289.4 0.7 copy-start.13
  290.1 2.4 copy-start.10
  290.8 2.4 copy-start.2
  290.8 2.4 copy-start.4
  292.5 1.4 copy-start.15
  296.3 8.6 %copy-start.14 = (f32[256,256]{1,0:T(8,128)S(1)}, f32[256,256]{1,0:T(8,128)}, u32[]{:S(2)}) copy-start(f32[256,256]{1,0:T(8,128)} %copy-done.13) | copy-start | bytes 786436
  296.3 105.5 %all-to-all-start.1 = ((bf16[2,32,32,1024]{3,2,0,1:T(8,128)(2,1)}), bf16[2,32,32,1024]{3,2,0,1:T(8,128)(2,1)}, u32[]{:S(2)}, u32[]{:S(2)}) async-start(bf16[2,32,32,1024]{3,2,0,1:T(8,128)(2,1)} %pad_maximum_fusion), calls=%async_computation.2 | async-start | bytes 8388608 | tf_op jit(solution)/shard_map/all_to_all | solution.py:134
Sparse Core Ops, SparseCore 0:
  10.5 52.4 reduce-scatter.1
